TPU v7x, 32 devices: a whole 2x2x4 slice. The times are simulated.
32 devices in a mesh: cfg: 2 (over y), space: 4 (over z), tm: 4 (over x, core).
Axes of the slice: x: 2, y: 2, z: 4, core: 2. Of those that a mesh axis runs over, the one named last changes fastest.
Arguments:
- solutions: bfloat16 [16, 128, 32, 3072], P(('cfg', 'tm'), None, None, 'space'), parts along dimension 0, may hold values from -6 to 6
- eigvecs: bfloat16 [16, 2, 128, 3072], P(('cfg', 'tm'), None, 'space'), parts along dimension 0, may hold values from -0.078125 to 0.078125
- source_time: int32 [256], P('cfg'), parts along dimension 0, may hold values from 0 to 7
Outputs:
- perambulator: bfloat16 [16, 128, 32, 128], P(('cfg', 'tm'), 'space'), parts along dimension 0
There are 2 independent parts, one for each index of `cfg`. A program takes and returns all parts, laid end to end along the dimension named above; each array names one. Nothing has to cross between parts.
All inputs are finite; a program needn't handle non-finite values.
Results may differ from a plain program's by a relative error of at most 0.001.
Values may be sent and summed in bfloat16 or wider, within the bound.
A program may use at most 128 MiB of HBM per device.

v0:
```python
import jax
import jax.numpy as jnp
from jax import lax
from jax.sharding import PartitionSpec as P


def contract_block(spinors, vectors):
    slices = spinors.shape[0]
    sources = spinors.shape[1]
    count = vectors.shape[2]
    stacked = vectors.reshape(slices, 2 * count, vectors.shape[3])
    products = jnp.einsum(
        "tkc,tjc->tkj",
        spinors.reshape(slices, sources * 32, spinors.shape[3]),
        stacked,
        preferred_element_type=jnp.float32,
    )
    products = products.reshape(slices, sources, 2, 16, 2, count)
    real_part = products[:, :, 0, :, 0, :] + products[:, :, 1, :, 1, :]
    imag_part = products[:, :, 1, :, 0, :] - products[:, :, 0, :, 1, :]
    return jnp.concatenate([real_part, imag_part], axis=2)


def shards(solutions, eigvecs, source_time):
    slices = solutions.shape[0]
    local_vectors = lax.all_to_all(eigvecs, "space", split_axis=3, concat_axis=2, tiled=True)
    partial_value = contract_block(solutions, local_vectors)
    sums = lax.psum_scatter(partial_value, "space", scatter_dimension=1, tiled=True)
    owned = sums.shape[1]
    first_source = lax.axis_index("space") * owned
    owned_times = lax.dynamic_slice_in_dim(source_time, first_source, owned)
    slice_index = lax.axis_index("tm") * slices + jnp.arange(slices, dtype=jnp.int32)
    signs = jnp.where(slice_index[:, None] < owned_times[None, :], -1.0, 1.0).astype(jnp.float32)
    return (sums * signs[:, :, None, None]).astype(jnp.bfloat16)


def solution(mesh):
    return jax.shard_map(
        shards,
        mesh=mesh,
        in_specs=(
            P(("cfg", "tm"), None, None, "space"),
            P(("cfg", "tm"), None, "space", None),
            P("cfg"),
        ),
        out_specs=P(("cfg", "tm"), "space", None, None),
        check_vma=False,
    )
```

profile of v0, /device:TPU:0, one launch (start us, length us, event | category | flops | bytes accessed | tf_op | source)
XLA Modules:
  0.0 179.1 jit_solution(6981386661717572682)
XLA Ops:
  6.5 0.0 reduce-scatter.5.cloned.1.call-start
  6.5 7.5 %copy.9 = bf16[2,2,32,3072]{2,1,0,3:T(2,128)(2,1)S(1)} copy(bf16[2,2,32,3072]{3,2,1,0:T(8,128)(2,1)} %param.4) | data formatting | bytes 1572864 | tf_op args[1]
  14.0 3.8 %reshape.48 = bf16[4,2,49152]{2,1,0:T(2,128)(2,1)} reshape(bf16[3072,2,2,32]{3,2,1,0:T(2,128)(2,1)S(1)} %bitcast.34) | data formatting | bytes 1572864
  17.8 26.6 %all_to_all.15 = bf16[4,2,49152]{2,1,0:T(2,128)(2,1)} all-to-all(bf16[4,2,49152]{2,1,0:T(2,128)(2,1)} %reshape.48), channel_id=1, replica_groups=mesh['cfg'=2,'space'=4,'tm'=4] {'space'}, dimensions={0} | all-to-all | bytes 1572864 | tf_op jit(solution)/shard_map/all_to_all | solution.py:26
  44.4 3.2 %reshape.49 = bf16[3072,2,2,32]{3,2,1,0:T(2,128)(2,1)S(1)} reshape(bf16[4,2,49152]{2,1,0:T(2,128)(2,1)} %all_to_all.15) | data formatting | bytes 1572864
  47.6 6.1 %copy.10 = bf16[2,2,32,4,768]{4,2,3,1,0:T(8,128)(2,1)} copy(bf16[2,2,32,4,768]{2,1,0,4,3:T(2,128)(2,1)S(1)} %bitcast.33) | data formatting | bytes 1572864 | tf_op jit(solution)/shard_map/all_to_all | solution.py:26
  53.7 11.4 %fusion.2 = f32[2,4096,256]{2,1,0:T(8,128)} fusion(bf16[2,4096,768]{2,1,0:T(8,128)(2,1)} %bitcast.32, bf16[2,256,768]{2,1,0:T(8,128)(2,1)} %bitcast.40), kind=kOutput, calls=%fused_computation.9 | convolution fusion | flops 3221225472 | bytes 21757952 | tf_op jit(solution)/shard_map/tkc,tjc->tkj/dot_general | solution.py:12
  65.1 10.8 %reshape.45 = f32[2,128,2,16,2,128]{5,4,3,2,1,0:T(2,128)} reshape(f32[2,4096,256]{2,1,0:T(8,128)} %fusion.2) | data formatting | bytes 16777216 | tf_op jit(solution)/shard_map/reshape | solution.py:18
  75.8 11.1 %fusion.1 = (f32[2,128,1,16,1,128]{5,4,3,2,1,0:T(1,128)S(1)}, f32[2,128,1,16,1,128]{5,4,3,2,1,0:T(1,128)S(1)}, f32[2,128,1,16,1,128]{5,4,3,2,1,0:T(1,128)S(1)}, f32[2,128,1,16,1,128]{5,4,3,2,1,0:T(1,128)S(1)}) fusion(f32[2,128,2,16,2,128]{5,4,3,2,1,0:T(2,128)} %reshape.45), kind=kLoop, calls=%fused_computation.8 | loop fusion | bytes 16777216 | tf_op jit(solution)/shard_map/slice | solution.py:19
  87.0 0.5 subtract_bitcast_fusion
  87.5 0.5 pad_maximum_fusion
  88.0 0.5 copy.15
  88.5 5.2 %copy.27 = f32[16,8,64,128]{3,1,2,0:T(8,128)} copy(f32[16,8,64,128]{3,2,1,0:T(8,128)S(1)} %bitcast.31) | data formatting | bytes 8388608
  93.8 0.0 copy-start
  93.8 0.0 reduce-scatter.5.cloned.1.call-update
  93.8 0.6 copy-done
  94.4 0.1 dynamic_slice.3
  94.5 0.1 compare_select_fusion
  94.6 75.3 %reduce-scatter.5.cloned.1.call-done = f32[32,8192]{1,0:T(8,128)} async-done(((f32[128,8192]{1,0:T(8,128)}), f32[32,8192]{1,0:T(8,128)}) %reduce-scatter.5.cloned.1.call-update) | async-done | bytes 1048592
  169.8 1.4 copy.22
  171.3 0.9 fusion
  (1 shorter events, 0.0 us)
Async XLA Ops:
  6.5 163.3 %reduce-scatter.5.cloned.1.call-start = ((), (), s32[]{:S(2)}) async-start(), calls=%async_computation.2 | async-start | bytes 5242880
  93.8 0.7 copy-start
Sparse Core Ops, SparseCore 0:
  93.9 75.8 reduce-scatter.4
where the time goes:
time: 180 us; the launch traced here: 179 us
  waiting for transfers between devices  75.3 us (42%)
  local copies, waits for them, and re-layouts  50.3 us (28%)
  blocking collectives  26.6 us (15%)
  between operations  13.5 us (8%)
  matrix products  11.4 us (6%)
  other arithmetic  2.09 us (1%)
    unnamed x2, waiting for transfers between devices  75.3 us
    all_to_all x1, blocking collectives, shards(): lax.all_to_all(eigvecs, 'space', split_axis=3, concat_axis=2, tiled=True)  26.6 us
    unnamed x8, local copies, waits for them, and re-layouts  22.2 us
    dot_general x1, matrix products, contract_block(): jnp.einsum('tkc,tjc->tkj', spinors.reshape(slices, sources * 32, spinors....  11.4 us
    slice x1, local copies, waits for them, and re-layouts, contract_block(): real_part = products[:, :, 0, :, 0, :] + products[:, :, 1, :, 1, :]  11.1 us
    reshape x1, local copies, waits for them, and re-layouts, contract_block(): products = products.reshape(slices, sources, 2, 16, 2, count)  10.8 us
    all_to_all x1, local copies, waits for them, and re-layouts, shards(): lax.all_to_all(eigvecs, 'space', split_axis=3, concat_axis=2, tiled=True)  6.11 us
  transfers between devices with their start and end apart: 1, of which 1 were waited for; matrix products, arithmetic and copies ran while one was open for 0% of the time, Pallas kernels for 0%

commit v1 on v0

--- a/solution.py
+++ b/solution.py
@@ -23,7 +23,12 @@
 
 def shards(solutions, eigvecs, source_time):
     slices = solutions.shape[0]
-    local_vectors = lax.all_to_all(eigvecs, "space", split_axis=3, concat_axis=2, tiled=True)
+    local_vectors = jnp.concatenate(
+        lax.all_to_all(
+            jnp.stack(jnp.split(eigvecs, lax.axis_size("space"), axis=3)), "space", 0, 0
+        ),
+        axis=2,
+    )
     partial_value = contract_block(solutions, local_vectors)
     sums = lax.psum_scatter(partial_value, "space", scatter_dimension=1, tiled=True)
     owned = sums.shape[1]

time: 180 us -> 172 us (0.956)
  local copies, waits for them, and re-layouts: 50.3 us -> 28.8 us
  other arithmetic: 2.09 us -> 12.9 us
  matrix products: 11.4 us -> 14.7 us
    unnamed x8 -> x5, local copies, waits for them, and re-layouts: 22.2 us -> 7.75 us
    slice x1 -> x0, local copies, waits for them, and re-layouts: 11.1 us -> none  [contract_block(): real_part = products[:, :, 0, :, 0, :] + products[:, :, 1, :, 1, :]]
    slice x0 -> x1, other arithmetic: none -> 10.9 us  [contract_block(): real_part = products[:, :, 0, :, 0, :] + products[:, :, 1, :, 1, :]]
    dot_general x0 -> x1, local copies, waits for them, and re-layouts: none -> 8.9 us  [contract_block(): jnp.einsum('tkc,tjc->tkj', spinors.reshape(slices, sources * 32, spinors....]
    all_to_all x1 -> x0, local copies, waits for them, and re-layouts: 6.11 us -> none  [shards(): lax.all_to_all(eigvecs, 'space', split_axis=3, concat_axis=2, tiled=True)]
    dot_general x1, matrix products: 11.4 us -> 14.7 us  [contract_block(): jnp.einsum('tkc,tjc->tkj', spinors.reshape(slices, sources * 32, spinors....]
where the time goes in v1:
time: 172 us; the launch traced here: 171 us
  waiting for transfers between devices  75.3 us (44%)
  local copies, waits for them, and re-layouts  28.8 us (17%)
  blocking collectives  26.3 us (15%)
  matrix products  14.7 us (9%)
  between operations  13.5 us (8%)
  other arithmetic  12.9 us (8%)
    unnamed x2, waiting for transfers between devices  75.3 us
    all_to_all x1, blocking collectives, shards(): lax.all_to_all(jnp.stack(jnp.split(eigvecs, lax.axis_size('space'), axis=...  26.3 us
    dot_general x1, matrix products, contract_block(): jnp.einsum('tkc,tjc->tkj', spinors.reshape(slices, sources * 32, spinors....  14.7 us
    slice x1, other arithmetic, contract_block(): real_part = products[:, :, 0, :, 0, :] + products[:, :, 1, :, 1, :]  10.9 us
    reshape x1, local copies, waits for them, and re-layouts, contract_block(): products = products.reshape(slices, sources, 2, 16, 2, count)  10.8 us
    dot_general x1, local copies, waits for them, and re-layouts, contract_block(): jnp.einsum('tkc,tjc->tkj', spinors.reshape(slices, sources * 32, spinors....  8.9 us
    unnamed x5, local copies, waits for them, and re-layouts  7.75 us
  transfers between devices with their start and end apart: 1, of which 1 were waited for; matrix products, arithmetic and copies ran while one was open for 0% of the time, Pallas kernels for 0%

profile of v1, /device:TPU:0, one launch (start us, length us, event | category | flops | bytes accessed | tf_op | source)
XLA Modules:
  0.0 171.4 jit_solution(1162986681444666037)
XLA Ops:
  6.5 0.0 reduce-scatter.5.cloned.1.call-start
  6.5 1.3 slice_bitcast_fusion.3
  7.8 0.1 pad_maximum_fusion.1
  7.9 26.3 %all_to_all.5 = bf16[4,2,2,32,768]{4,3,2,1,0:T(8,128)(2,1)S(1)} all-to-all(bf16[4,2,2,32,768]{4,3,2,1,0:T(8,128)(2,1)S(1)} %pad_maximum_fusion.1), channel_id=1, replica_groups=mesh['cfg'=2,'space'=4,'tm'=4] {'space'}, dimensions={0} | all-to-all | bytes 1572864 | tf_op jit(solution)/shard_map/all_to_all | solution.py:27
  34.2 0.1 copy.13
  34.2 14.7 %convolution_bitcast_fusion = f32[2,4096,256]{1,2,0:T(8,128)} fusion(bf16[2,256,768]{2,1,0:T(8,128)(2,1)S(1)} %bitcast.41, bf16[2,4096,768]{2,1,0:T(8,128)(2,1)} %bitcast.35), kind=kOutput, calls=%fused_computation | convolution fusion | flops 3221225472 | bytes 21757952 | tf_op jit(solution)/shard_map/tkc,tjc->tkj/dot_general | solution.py:12
  48.9 8.9 %copy.14 = f32[2,4096,256]{2,1,0:T(8,128)} copy(f32[2,4096,256]{1,2,0:T(8,128)} %convolution_bitcast_fusion) | data formatting | bytes 16777216 | tf_op jit(solution)/shard_map/tkc,tjc->tkj/dot_general | solution.py:12
  57.8 10.8 %reshape.44 = f32[2,128,2,16,2,128]{5,4,3,2,1,0:T(2,128)} reshape(f32[2,4096,256]{2,1,0:T(8,128)} %copy.14) | data formatting | bytes 16777216 | tf_op jit(solution)/shard_map/reshape | solution.py:18
  68.6 10.9 %fusion.1 = (f32[2,128,1,16,1,128]{5,4,3,2,1,0:T(1,128)S(1)}, f32[2,128,1,16,1,128]{5,4,3,2,1,0:T(1,128)S(1)}, f32[2,128,1,16,1,128]{5,4,3,2,1,0:T(1,128)S(1)}) fusion(f32[2,128,2,16,2,128]{5,4,3,2,1,0:T(2,128)} %reshape.44), kind=kLoop, calls=%fused_computation.14 | loop fusion | flops 524288 | bytes 14680064 | tf_op jit(solution)/shard_map/slice | solution.py:19
  79.5 0.3 add_bitcast_fusion
  79.7 0.6 pad_maximum_fusion
  80.4 0.5 copy.17
  80.9 5.2 %copy.27 = f32[16,8,64,128]{3,1,2,0:T(8,128)} copy(f32[16,8,64,128]{3,2,1,0:T(8,128)S(1)} %bitcast.34) | data formatting | bytes 8388608
  86.1 0.0 copy-start
  86.1 0.0 reduce-scatter.5.cloned.1.call-update
  86.1 0.6 copy-done
  86.8 0.1 dynamic_slice.3
  86.8 0.1 compare_select_fusion
  86.9 75.3 %reduce-scatter.5.cloned.1.call-done = f32[32,8192]{1,0:T(8,128)} async-done(((f32[128,8192]{1,0:T(8,128)}), f32[32,8192]{1,0:T(8,128)}) %reduce-scatter.5.cloned.1.call-update) | async-done | bytes 1048592
  162.2 1.4 copy.22
  163.6 0.9 fusion
  (1 shorter events, 0.0 us)
Async XLA Ops:
  6.5 155.7 %reduce-scatter.5.cloned.1.call-start = ((), (), s32[]{:S(2)}) async-start(), calls=%async_computation.2 | async-start | bytes 5242880
  86.1 0.7 copy-start
Sparse Core Ops, SparseCore 0:
  86.3 75.8 reduce-scatter.4
